TPU v7x, 32 devices: a whole 2x2x4 slice. The times are simulated.
32 devices in a mesh: seq: 8 (over y, x, core), head: 4 (over z).
Axes of the slice: x: 2, y: 2, z: 4, core: 2. Of those that a mesh axis runs over, the one named last changes fastest.
Arguments:
- tokens: bfloat16 [32, 1024, 1024], P('seq'), may hold values from -6 to 6
- w_query: bfloat16 [1024, 1024], P(None, 'head'), may hold values from -1 to 1
- w_key: bfloat16 [1024, 1024], P(None, 'head'), may hold values from -1 to 1
- w_value: bfloat16 [1024, 1024], P(None, 'head'), may hold values from -0.1875 to 0.1875
- w_out: bfloat16 [1024, 1024], P('head'), may hold values from -0.1875 to 0.1875
Outputs:
- mixed: bfloat16 [32, 1024, 1024], P('seq', None, 'head')
All inputs are finite; a program needn't handle non-finite values.
Results may differ from a plain program's by a relative error of at most 0.012.
Values may be sent and summed in bfloat16 or wider, within the bound.
No kernel may reach another device: no remote copies, remote signals or barrier semaphores. Data moves between devices by JAX's collectives and lax.ppermute only.
A program may use at most 128 MiB of HBM per device.

v0:
```python
import jax
import jax.numpy as jnp
from jax import lax
from jax.sharding import PartitionSpec as P

HS = 64


epsilon = 1e-05


def normalize(tokens):
    values = tokens.astype(jnp.float32)
    row_mean = jnp.mean(values, axis=-1, keepdims=True)
    centered = values - row_mean
    row_var = jnp.mean(centered * centered, axis=-1, keepdims=True)
    return (centered * lax.rsqrt(row_var + epsilon)).astype(jnp.bfloat16)


def project(source, weight):
    return jnp.einsum("fpd,dc->fpc", source, weight, preferred_element_type=jnp.float32).astype(
        jnp.bfloat16
    )


def attend(queries, key_rows, value_rows, head_count):
    frames, patch_count, feature_width = queries.shape
    head_size = feature_width // head_count
    query_flat = queries.reshape(frames, patch_count * head_count, head_size)
    key_flat = key_rows.reshape(frames, patch_count * head_count, head_size)
    value_flat = value_rows.reshape(frames, patch_count * head_count, head_size)
    scores = jnp.einsum(
        "fmd,gmd->fgm", query_flat, key_flat, preferred_element_type=jnp.float32
    ) * head_size ** (-0.5)
    row_top = jnp.max(scores, axis=1, keepdims=True)
    raised = jnp.exp(scores - row_top)
    weights = (raised / jnp.sum(raised, axis=1, keepdims=True)).astype(jnp.bfloat16)
    attended = jnp.einsum("fgm,gmd->fmd", weights, value_flat, preferred_element_type=jnp.float32)
    return attended.astype(jnp.bfloat16).reshape(frames, patch_count, feature_width)


def local(tokens, w_query, w_key, w_value, w_out):
    normed = normalize(tokens)
    head_count = w_query.shape[1] // HS
    local_query = project(normed, w_query)
    local_key = project(normed, w_key)
    local_value = project(normed, w_value)
    queries, key_rows, value_rows = (
        lax.all_to_all(local_query, "seq", split_axis=1, concat_axis=0, tiled=True),
        lax.all_to_all(local_key, "seq", split_axis=1, concat_axis=0, tiled=True),
        lax.all_to_all(local_value, "seq", split_axis=1, concat_axis=0, tiled=True),
    )
    attended = attend(queries, key_rows, value_rows, head_count)
    partial_value = jnp.einsum("fpc,cd->fpd", attended, w_out, preferred_element_type=jnp.float32)
    columns = lax.psum_scatter(
        partial_value.astype(jnp.bfloat16), "head", scatter_dimension=2, tiled=True
    )
    return lax.all_to_all(columns, "seq", split_axis=0, concat_axis=1, tiled=True)


def solution(mesh):
    return jax.shard_map(
        local,
        mesh=mesh,
        in_specs=(
            P("seq", None, None),
            P(None, "head"),
            P(None, "head"),
            P(None, "head"),
            P("head", None),
        ),
        out_specs=P("seq", None, "head"),
        check_vma=False,
    )
```

profile of v0, /device:TPU:0, one launch (start us, length us, event | category | flops | bytes accessed | tf_op | source)
XLA Modules:
  0.0 326.3 jit_solution(13314724638309537397)
XLA Ops:
  6.5 0.0 copy-start
  6.5 0.0 copy-start.1
  6.5 0.0 copy-start.3
  6.5 4.7 %convert_reduce_fusion = f32[4,1024]{1,0:T(4,128)S(1)} fusion(bf16[4,1024,1024]{2,1,0:T(8,128)(2,1)} %param.5), kind=kLoop, calls=%fused_computation.2 | loop fusion | flops 8384512 | bytes 8404992 | tf_op jit(solution)/shard_map/reduce_sum | solution.py:14
  11.3 1.1 copy-done.1
  12.4 2.8 fusion.3
  15.2 0.0 copy-done.3
  15.2 3.1 fusion.28
  18.3 0.0 copy-start.4
  18.4 3.0 copy.19
  21.3 5.2 %all-to-all-start.1 = ((bf16[4,1024,256]{2,0,1:T(4,128)(2,1)}), bf16[4,1024,256]{2,0,1:T(4,128)(2,1)S(1)}, u32[]{:S(2)}, u32[]{:S(2)}) async-start(bf16[4,1024,256]{2,0,1:T(4,128)(2,1)} %copy.19), calls=%async_computation.1 | async-start | bytes 4194304 | tf_op jit(solution)/shard_map/all_to_all | solution.py:50
  26.5 0.0 copy-done.4
  26.5 5.0 %fusion.31 = bf16[4,1024,256]{2,1,0:T(8,128)(2,1)S(1)} fusion(bf16[4,1024,1024]{2,1,0:T(8,128)(2,1)} %param.5, f32[4,1024]{1,0:T(4,128)S(1)} %add_rsqrt_fusion, f32[4,1024]{1,0:T(4,128)S(1)} %broadcast_multiply_fusion, bf16[1024,256]{1,0:T(8,128)(2,1)S(1)} %copy-done.4), kind=kOutput, calls=%fused_computation.30 | convolution fusion | flops 2165309440 | bytes 11042816 | tf_op jit(solution)/shard_map/fpd,dc->fpc/dot_general | solution.py:21
  31.5 0.0 copy-start.5
  31.6 2.9 copy.21
  34.5 18.6 %all-to-all-done.1 = bf16[4,1024,256]{2,0,1:T(4,128)(2,1)S(1)} async-done(((bf16[4,1024,256]{2,0,1:T(4,128)(2,1)}), bf16[4,1024,256]{2,0,1:T(4,128)(2,1)S(1)}, u32[]{:S(2)}, u32[]{:S(2)}) %all-to-all-start.1) | async-done | bytes 2097184 | tf_op jit(solution)/shard_map/all_to_all | solution.py:50
  53.1 0.0 copy-start.2
  53.1 4.3 %all-to-all-start.2 = ((bf16[4,1024,256]{2,0,1:T(4,128)(2,1)}), bf16[4,1024,256]{2,0,1:T(4,128)(2,1)}, u32[]{:S(2)}, u32[]{:S(2)}) async-start(bf16[4,1024,256]{2,0,1:T(4,128)(2,1)} %copy.21), calls=%async_computation.2 | async-start | bytes 4194304 | tf_op jit(solution)/shard_map/all_to_all | solution.py:49
  57.5 0.0 copy-done.5
  57.5 5.0 %fusion.25 = bf16[4,1024,256]{2,1,0:T(8,128)(2,1)S(1)} fusion(bf16[4,1024,1024]{2,1,0:T(8,128)(2,1)} %param.5, f32[4,1024]{1,0:T(4,128)S(1)} %add_rsqrt_fusion, f32[4,1024]{1,0:T(4,128)S(1)} %broadcast_multiply_fusion, bf16[1024,256]{1,0:T(8,128)(2,1)S(1)} %copy-done.5), kind=kOutput, calls=%fused_computation.28 | convolution fusion | flops 2165309440 | bytes 11042816 | tf_op jit(solution)/shard_map/fpd,dc->fpc/dot_general | solution.py:21
  62.5 0.0 copy-done.2
  62.5 2.9 copy.17
  65.5 18.7 %all-to-all-done.2 = bf16[4,1024,256]{2,0,1:T(4,128)(2,1)} async-done(((bf16[4,1024,256]{2,0,1:T(4,128)(2,1)}), bf16[4,1024,256]{2,0,1:T(4,128)(2,1)}, u32[]{:S(2)}, u32[]{:S(2)}) %all-to-all-start.2) | async-done | bytes 2097184 | tf_op jit(solution)/shard_map/all_to_all | solution.py:49
  84.1 4.4 %all-to-all-start = ((bf16[4,1024,256]{2,0,1:T(4,128)(2,1)}), bf16[4,1024,256]{2,0,1:T(4,128)(2,1)}, u32[]{:S(2)}, u32[]{:S(2)}) async-start(bf16[4,1024,256]{2,0,1:T(4,128)(2,1)} %copy.17), calls=%async_computation | async-start | bytes 4194304 | tf_op jit(solution)/shard_map/all_to_all | solution.py:51
  88.5 0.2 reduce-scatter.2.cloned.1.call-start
  88.7 2.0 copy.42
  90.7 3.3 reshape.30
  94.0 2.0 copy.41
  95.9 3.2 reshape.31
  99.2 8.3 %fusion.18 = f32[512,32,32]{2,1,0:T(8,128)S(1)} fusion(bf16[32,512,64]{2,1,0:T(8,128)(2,1)} %reshape.31, bf16[32,512,64]{2,1,0:T(8,128)(2,1)} %reshape.30), kind=kOutput, calls=%fused_computation.19 | convolution fusion | flops 67108864 | bytes 6291456 | tf_op jit(solution)/shard_map/fmd,gmd->fgm/dot_general | solution.py:32
  107.5 6.1 %fusion.39 = (f32[32,512]{0,1:T(8,128)S(1)}, f32[32,32,512]{0,1,2:T(8,128)}) fusion(f32[512,32,32]{2,1,0:T(8,128)S(1)} %fusion.18), kind=kOutput, calls=%fused_computation.38 | output fusion | flops 2097183 | bytes 4259840 | tf_op jit(solution)/shard_map/sub | solution.py:36
  113.6 1.5 all-to-all-done
  115.1 2.0 copy.43
  117.1 3.3 %reshape.29 = bf16[32,512,64]{2,1,0:T(8,128)(2,1)} reshape(bf16[8,4,128,256]{3,2,1,0:T(8,128)(2,1)S(1)} %bitcast.50) | data formatting | bytes 4194304 | tf_op jit(solution)/shard_map/reshape | solution.py:31
  120.4 8.1 %convert_bitcast_fusion = bf16[32,512,64]{2,0,1:T(8,128)(2,1)S(1)} fusion(f32[32,32,512]{0,1,2:T(8,128)} %get-tuple-element.6, f32[32,512]{0,1:T(8,128)S(1)} %get-tuple-element.5, bf16[32,512,64]{2,1,0:T(8,128)(2,1)} %reshape.29), kind=kOutput, calls=%fused_computation.22 | convolution fusion | flops 69206016 | bytes 6356992 | tf_op jit(solution)/shard_map/fgm,gmd->fmd/dot_general | solution.py:38
  128.5 3.6 %copy.27 = bf16[32,512,64]{2,1,0:T(8,128)(2,1)} copy(bf16[32,512,64]{2,0,1:T(8,128)(2,1)S(1)} %convert_bitcast_fusion) | data formatting | bytes 4194304 | tf_op jit(solution)/shard_map/convert_element_type | solution.py:39
  132.1 5.5 %reshape.32 = bf16[32,128,256]{2,1,0:T(8,128)(2,1)S(1)} reshape(bf16[32,512,64]{2,1,0:T(8,128)(2,1)} %copy.27) | data formatting | bytes 4194304 | tf_op jit(solution)/shard_map/reshape | solution.py:39
  137.6 0.0 copy-done
  137.6 5.6 %convolution_convert_fusion = bf16[32,128,1024]{2,1,0:T(8,128)(2,1)} fusion(bf16[32,128,256]{2,1,0:T(8,128)(2,1)S(1)} %reshape.32, bf16[256,1024]{1,0:T(8,128)(2,1)S(1)} %copy-done), kind=kOutput, calls=%fused_computation.13 | convolution fusion | flops 2151677952 | bytes 11010048 | tf_op jit(solution)/shard_map/fpc,cd->fpd/dot_general | solution.py:54
  143.1 0.0 reduce-scatter.2.cloned.1.call-update
  143.2 144.7 %reduce-scatter.2.cloned.1.call-done = bf16[32,128,256]{2,1,0:T(8,128)(2,1)} async-done(((bf16[32,128,1024]{2,1,0:T(8,128)(2,1)}), bf16[32,128,256]{2,1,0:T(8,128)(2,1)}) %reduce-scatter.2.cloned.1.call-update) | async-done | bytes 2097168 | tf_op jit(solution)/shard_map/reduce_scatter | solution.py:55
  287.8 30.2 %all_to_all.63 = bf16[32,128,256]{2,1,0:T(8,128)(2,1)S(1)} all-to-all(bf16[32,128,256]{2,1,0:T(8,128)(2,1)} %reduce-scatter.2.cloned.1.call-done), channel_id=1, replica_groups=mesh['seq'=8,'head'=4] {'seq'}, dimensions={0} | all-to-all | bytes 4194304 | tf_op jit(solution)/shard_map/all_to_all | solution.py:58
  318.0 1.5 copy.28
  (2 shorter events, 0.0 us)
Async XLA Ops:
  6.5 131.0 %copy-start = (bf16[256,1024]{1,0:T(8,128)(2,1)S(1)}, bf16[256,1024]{1,0:T(8,128)(2,1)}, u32[]{:S(2)}) copy-start(bf16[256,1024]{1,0:T(8,128)(2,1)} %param.9) | copy-start | bytes 1572868
  6.5 5.8 %copy-start.1 = (bf16[4,1024,1024]{2,1,0:T(8,128)(2,1)S(1)}, bf16[4,1024,1024]{2,1,0:T(8,128)(2,1)}, u32[]{:S(2)}) copy-start(bf16[4,1024,1024]{2,1,0:T(8,128)(2,1)} %param.5) | copy-start | bytes 25165828
  6.5 8.6 %copy-start.3 = (bf16[1024,256]{1,0:T(8,128)(2,1)S(1)}, bf16[1024,256]{1,0:T(8,128)(2,1)}, u32[]{:S(2)}) copy-start(bf16[1024,256]{1,0:T(8,128)(2,1)} %param.7) | copy-start | bytes 1572868
  18.3 8.2 %copy-start.4 = (bf16[1024,256]{1,0:T(8,128)(2,1)S(1)}, bf16[1024,256]{1,0:T(8,128)(2,1)}, u32[]{:S(2)}) copy-start(bf16[1024,256]{1,0:T(8,128)(2,1)} %param.6) | copy-start | bytes 1572868
  21.3 31.8 %all-to-all-start.1 = ((bf16[4,1024,256]{2,0,1:T(4,128)(2,1)}), bf16[4,1024,256]{2,0,1:T(4,128)(2,1)S(1)}, u32[]{:S(2)}, u32[]{:S(2)}) async-start(bf16[4,1024,256]{2,0,1:T(4,128)(2,1)} %copy.19), calls=%async_computation.1 | async-start | bytes 4194304 | tf_op jit(solution)/shard_map/all_to_all | solution.py:50
  31.5 25.9 %copy-start.5 = (bf16[1024,256]{1,0:T(8,128)(2,1)S(1)}, bf16[1024,256]{1,0:T(8,128)(2,1)}, u32[]{:S(2)}) copy-start(bf16[1024,256]{1,0:T(8,128)(2,1)} %param.8) | copy-start | bytes 1572868
  53.1 9.4 %copy-start.2 = (bf16[4,1024,256]{2,0,1:T(4,128)(2,1)}, bf16[4,1024,256]{2,0,1:T(4,128)(2,1)S(1)}, u32[]{:S(2)}) copy-start(bf16[4,1024,256]{2,0,1:T(4,128)(2,1)S(1)} %all-to-all-done.1) | copy-start | bytes 6291460
  53.1 31.0 %all-to-all-start.2 = ((bf16[4,1024,256]{2,0,1:T(4,128)(2,1)}), bf16[4,1024,256]{2,0,1:T(4,128)(2,1)}, u32[]{:S(2)}, u32[]{:S(2)}) async-start(bf16[4,1024,256]{2,0,1:T(4,128)(2,1)} %copy.21), calls=%async_computation.2 | async-start | bytes 4194304 | tf_op jit(solution)/shard_map/all_to_all | solution.py:49
  84.1 31.0 %all-to-all-start = ((bf16[4,1024,256]{2,0,1:T(4,128)(2,1)}), bf16[4,1024,256]{2,0,1:T(4,128)(2,1)}, u32[]{:S(2)}, u32[]{:S(2)}) async-start(bf16[4,1024,256]{2,0,1:T(4,128)(2,1)} %copy.17), calls=%async_computation | async-start | bytes 4194304 | tf_op jit(solution)/shard_map/all_to_all | solution.py:51
  88.5 199.3 %reduce-scatter.2.cloned.1.call-start = ((), (), s32[]{:S(2)}) async-start(), calls=%async_computation.5 | async-start | bytes 10485760 | tf_op jit(solution)/shard_map/reduce_scatter | solution.py:55
Sparse Core Ops, SparseCore 0:
  143.3 144.4 reduce-scatter.1
where the time goes:
time: 327 us; the launch traced here: 326 us
  waiting for transfers between devices  184 us (56%)
  local copies, waits for them, and re-layouts  36.1 us (11%)
  matrix products  35.2 us (11%)
  blocking collectives  30.2 us (9%)
  starting transfers between devices  14.1 us (4%)
  other arithmetic  13.6 us (4%)
  between operations  13.6 us (4%)
    reduce_scatter x1, waiting for transfers between devices, local(): lax.psum_scatter(partial_value.astype(jnp.bfloat16), 'head', scatter_dime...  145 us
    all_to_all x1, blocking collectives, local(): lax.all_to_all(columns, 'seq', split_axis=0, concat_axis=1, tiled=True)  30.2 us
    all_to_all x1, waiting for transfers between devices, local(): lax.all_to_all(local_query, 'seq', split_axis=1, concat_axis=0, tiled=True)  18.7 us
    all_to_all x1, waiting for transfers between devices, local(): lax.all_to_all(local_key, 'seq', split_axis=1, concat_axis=0, tiled=True)  18.6 us
    dot_general x3, matrix products, project(): jnp.einsum('fpd,dc->fpc', source, weight, preferred_element_type=jnp.floa...  13.2 us
    convert_element_type x3, local copies, waits for them, and re-layouts, project(): jnp.einsum('fpd,dc->fpc', source, weight, preferred_element_type=jnp.floa...  8.83 us
    dot_general x1, matrix products, attend(): jnp.einsum('fmd,gmd->fgm', query_flat, key_flat, preferred_element_type=j...  8.29 us
    dot_general x1, matrix products, attend(): jnp.einsum('fgm,gmd->fmd', weights, value_flat, preferred_element_type=jn...  8.14 us
  transfers between devices with their start and end apart: 4, of which 4 were waited for; matrix products, arithmetic and copies ran while one was open for 12% of the time, Pallas kernels for 0%

commit v1 on v0

v1 whole, which is shorter than its diff:
```python
import functools

import jax
import jax.numpy as jnp
from jax import lax
from jax.experimental import pallas as pl
from jax.experimental.pallas import tpu as pltpu
from jax.sharding import PartitionSpec as P

HS = 64
GROUP = 4
LANES = 128

epsilon = 1e-05


def block_kernel(x_ref, w_ref, o_ref, *, groups):
    width = x_ref.shape[-1]
    heads, seq, rows, packed = w_ref.shape
    cols = packed // 4
    splits = seq // heads
    count = x_ref.shape[0] * x_ref.shape[2]
    x = jnp.concatenate([x_ref[:, g].reshape(count, width) for g in range(groups)], axis=0)
    values = x.astype(jnp.float32)
    centered = values - jnp.mean(values, axis=-1, keepdims=True)
    row_var = jnp.mean(centered * centered, axis=-1, keepdims=True)
    normed = (centered * lax.rsqrt(row_var + epsilon)).astype(jnp.bfloat16)
    row = lax.broadcasted_iota(jnp.int32, (2 * count, count), 0)
    col = lax.broadcasted_iota(jnp.int32, (2 * count, count), 1)
    same = (row % GROUP) == (col % GROUP)
    lane = lax.broadcasted_iota(jnp.int32, (count, LANES), 1)
    first = lane < HS
    attended = []
    for h in range(heads):
        weight = w_ref[h].reshape(seq * rows, packed)[:, : 3 * cols]
        qkv = jnp.dot(normed, weight, preferred_element_type=jnp.float32).astype(jnp.bfloat16)
        for pair in range(cols // LANES):
            parts = []
            for g in range(groups):
                span = slice(g * count, (g + 1) * count)
                at = pair * LANES
                q = qkv[span, at : at + LANES] * jnp.bfloat16(HS ** (-0.5))
                k = qkv[span, cols + at : cols + at + LANES]
                v = qkv[span, 2 * cols + at : 2 * cols + at + LANES]
                zero = jnp.zeros_like(q)
                both = jnp.concatenate([jnp.where(first, q, zero), jnp.where(first, zero, q)], axis=0)
                scores = lax.dot_general(
                    both, k, (((1,), (1,)), ((), ())), preferred_element_type=jnp.float32
                )
                scores = jnp.where(same, scores, -1e30)
                raised = jnp.exp(scores - jnp.max(scores, axis=1, keepdims=True))
                weights = (raised / jnp.sum(raised, axis=1, keepdims=True)).astype(jnp.bfloat16)
                out = jnp.dot(weights, v, preferred_element_type=jnp.float32)
                parts.append(jnp.where(first, out[:count], out[count:]).astype(jnp.bfloat16))
            attended.append(jnp.concatenate(parts, axis=0))
    attended = jnp.concatenate(attended, axis=1)
    for c in range(heads):
        total = None
        for h in range(heads):
            block = w_ref[h, c * splits : (c + 1) * splits, :, 3 * cols :].reshape(splits * rows, cols)
            piece = jnp.dot(
                attended[:, h * cols : (h + 1) * cols], block, preferred_element_type=jnp.float32
            )
            total = piece if total is None else total + piece
        mixed = total.astype(jnp.bfloat16)
        for g in range(groups):
            o_ref[:, c, g] = mixed[g * count : (g + 1) * count].reshape(o_ref.shape[0], -1, cols)


def block(x, weights, groups):
    sources, total, rows, width = x.shape
    heads, seq, _, packed = weights.shape
    cols = packed // 4
    return pl.pallas_call(
        functools.partial(block_kernel, groups=groups),
        grid=(total // groups,),
        in_specs=[
            pl.BlockSpec((sources, groups, rows, width), lambda i: (0, i, 0, 0)),
            pl.BlockSpec(weights.shape, lambda i: (0, 0, 0, 0), pipeline_mode=pl.Buffered(1)),
        ],
        out_specs=pl.BlockSpec((sources, heads, groups, rows, cols), lambda i: (0, 0, i, 0, 0)),
        out_shape=jax.ShapeDtypeStruct((sources, heads, total, rows, cols), jnp.bfloat16),
        compiler_params=pltpu.CompilerParams(vmem_limit_bytes=56 * 1024 * 1024),
        cost_estimate=pl.CostEstimate(flops=10 * 2**30, transcendentals=2**21, bytes_accessed=12 * 2**20),
    )(x, weights)


def gather_weights(w_query, w_key, w_value, w_out, seq, head):
    s = lax.axis_index("seq")
    width, cols = w_query.shape
    rows = width // seq
    take = lambda w: lax.dynamic_slice_in_dim(w, s * rows, rows, 0)
    per_block = w_out.shape[0] // rows
    out = lax.dynamic_slice(w_out, ((s % per_block) * rows, (s // per_block) * cols), (rows, cols))
    mine = jnp.concatenate([take(w_query), take(w_key), take(w_value), out], axis=1)
    return lax.all_gather(mine, ("head", "seq"), axis=0, tiled=False).reshape(head, seq, rows, 4 * cols)


def local(seq, head, tokens, w_query, w_key, w_value, w_out):
    frames, patches, width = tokens.shape
    mine = patches // (seq * head)
    total = mine // GROUP
    rows = frames * GROUP
    weights = gather_weights(w_query, w_key, w_value, w_out, seq, head)
    h = lax.axis_index("head")
    x = tokens.reshape(frames, seq, head, mine, width)
    x = lax.dynamic_index_in_dim(x, h, axis=2, keepdims=False)
    x = x.reshape(frames, seq, total, GROUP, width)
    x = x.transpose(1, 2, 0, 3, 4).reshape(seq, total, rows, width)
    x = lax.all_to_all(x, "seq", split_axis=0, concat_axis=0, tiled=True)
    direct = rows % 16 == 0
    if not direct:
        x = x.transpose(1, 0, 2, 3).reshape(1, total, seq * rows, width)
    y = block(x, weights, 2)
    cols = y.shape[-1]
    if not direct:
        y = y.reshape(head, total, seq, rows, cols).transpose(2, 0, 1, 3, 4)
    y = y.reshape(seq * head, total * rows, cols)
    y = lax.all_to_all(y, ("seq", "head"), split_axis=0, concat_axis=0, tiled=True)
    y = y.reshape(seq * head, total, frames, GROUP, cols).transpose(2, 0, 1, 3, 4)
    return y.reshape(frames, patches, cols)


def solution(mesh):
    return jax.shard_map(
        functools.partial(local, mesh.shape["seq"], mesh.shape["head"]),
        mesh=mesh,
        in_specs=(
            P("seq", None, None),
            P(None, "head"),
            P(None, "head"),
            P(None, "head"),
            P("head", None),
        ),
        out_specs=P("seq", None, "head"),
        check_vma=False,
    )
```

time: 327 us -> 198 us (0.61)
  waiting for transfers between devices: 184 us -> 41.6 us
  blocking collectives: 30.2 us -> 89.5 us
  matrix products: 35.2 us -> 0 us
  Pallas kernels: 0 us -> 34.6 us
  local copies, waits for them, and re-layouts: 36.1 us -> 16.2 us
  starting transfers between devices: 14.1 us -> 0.01 us
  other arithmetic: 13.6 us -> 0.73 us
    reduce_scatter x1 -> x0, waiting for transfers between devices: 145 us -> none  [local(): lax.psum_scatter(partial_value.astype(jnp.bfloat16), 'head', scatter_dime...]
    all_to_all x1 -> x2, blocking collectives: 30.2 us -> 89.5 us  [the longest x1 50.6 us: local(): lax.all_to_all(y, ('seq', 'head'), split_axis=0, concat_axis=0, tiled=True)]
    all_gather x0 -> x1, waiting for transfers between devices: none -> 41.6 us  [gather_weights(): lax.all_gather(mine, ('head', 'seq'), axis=0, tiled=False)]
    all_to_all x3 -> x0, waiting for transfers between devices: 38.8 us -> none  [the longest x1 18.7 us: local(): lax.all_to_all(local_query, 'seq', split_axis=1, concat_axis=0, tiled=True)]
    dot_general x6 -> x0, matrix products: 35.2 us -> none  [the longest x3 13.2 us: project(): jnp.einsum('fpd,dc->fpc', source, weight, preferred_element_type=jnp.floa...]
    pallas_call x0 -> x1, Pallas kernels: none -> 34.6 us  [block(): pl.pallas_call(functools.partial(block_kernel, groups=groups), grid=(tota...]
    all_to_all x3 -> x0, starting transfers between devices: 13.9 us -> none  [the longest x1 5.21 us: local(): lax.all_to_all(local_key, 'seq', split_axis=1, concat_axis=0, tiled=True)]
    convert_element_type x4 -> x0, local copies, waits for them, and re-layouts: 12.4 us -> none  [the longest x3 8.83 us: project(): jnp.einsum('fpd,dc->fpc', source, weight, preferred_element_type=jnp.floa...]
  transfers between devices with their start and end apart: 4 -> 1, of which waited for: 4 -> 1; matrix products, arithmetic and copies ran while one was open for 12% -> 3% of each run, Pallas kernels for 0% -> 0%
where the time goes in v1:
time: 198 us; the launch traced here: 196 us
  blocking collectives  89.5 us (45%)
  waiting for transfers between devices  41.6 us (21%)
  Pallas kernels  34.6 us (17%)
  local copies, waits for them, and re-layouts  16.2 us (8%)
  between operations  13.4 us (7%)
    all_to_all x1, blocking collectives, local(): lax.all_to_all(y, ('seq', 'head'), split_axis=0, concat_axis=0, tiled=True)  50.6 us
    all_gather x1, waiting for transfers between devices, gather_weights(): lax.all_gather(mine, ('head', 'seq'), axis=0, tiled=False)  41.6 us
    all_to_all x1, blocking collectives, local(): x = lax.all_to_all(x, 'seq', split_axis=0, concat_axis=0, tiled=True)  38.8 us
    pallas_call x1, Pallas kernels, block(): pl.pallas_call(functools.partial(block_kernel, groups=groups), grid=(tota...  34.6 us
    reshape x2, local copies, waits for them, and re-layouts, local(): y.reshape(seq * head, total, frames, GROUP, cols).transpose(2, 0, 1, 3, 4)  4.78 us
  transfers between devices with their start and end apart: 1, of which 1 were waited for; matrix products, arithmetic and copies ran while one was open for 3% of the time, Pallas kernels for 0%

profile of v1, /device:TPU:0, one launch (start us, length us, event | category | flops | bytes accessed | tf_op | source)
XLA Modules:
  0.0 196.0 jit_solution(2873507701062999415)
XLA Ops:
  6.5 0.0 copy-start
  6.5 0.0 all-gather.3.cloned.1.call-start
  6.5 1.0 copy-done
  7.6 0.9 constant_dynamic-slice_fusion
  8.5 0.9 dynamic_slice.20
  9.3 0.7 pad_maximum_fusion
  10.0 0.0 all-gather.3.cloned.1.call-update
  10.1 1.8 constant_dynamic-slice_fusion.3
  11.9 1.2 copy.9
  13.0 1.6 copy.10
  14.6 2.0 %reshape.24 = bf16[8,8,16,1024]{3,2,1,0:T(8,128)(2,1)} reshape(bf16[8,8,4,4,1024]{4,3,2,1,0:T(4,128)(2,1)S(1)} %copy.10) | data formatting | bytes 4194304 | tf_op jit(solution)/shard_map/reshape | solution.py:109
  16.7 38.8 %all_to_all.10.x_ref = bf16[8,8,16,1024]{3,2,1,0:T(8,128)(2,1)} all-to-all(bf16[8,8,16,1024]{3,2,1,0:T(8,128)(2,1)} %reshape.24), channel_id=1, replica_groups=mesh['seq'=8,'head'=4] {'seq'}, dimensions={0} | all-to-all | bytes 4194304 | tf_op jit(solution)/shard_map/all_to_all | solution.py:110
  55.5 41.6 %all-gather.3.cloned.1.call-done = bf16[4096,1024]{1,0:T(8,128)(2,1)} async-done(((bf16[128,1024]{1,0:T(8,128)(2,1)}), bf16[4096,1024]{1,0:T(8,128)(2,1)}) %all-gather.3.cloned.1.call-update) | async-done | bytes 8388624 | tf_op jit(solution)/shard_map/all_gather | solution.py:96
  97.0 34.6 %shard_map.55 = bf16[8,4,8,16,256]{4,3,2,1,0:T(8,128)(2,1)} custom-call(bf16[8,8,16,1024]{3,2,1,0:T(8,128)(2,1)} %all_to_all.10.x_ref, bf16[4,8,128,1024]{3,2,1,0:T(8,128)(2,1)} %bitcast.13), custom_call_target="tpu_custom_call" | custom-call | flops 10737418240 | bytes 12582912 | tf_op jit(solution)/shard_map/pallas_call | solution.py:74
  131.7 50.6 %all_to_all.11 = bf16[32,128,256]{2,1,0:T(8,128)(2,1)S(1)} all-to-all(bf16[32,128,256]{2,1,0:T(8,128)(2,1)} %bitcast.11), channel_id=1, replica_groups=mesh['seq'=8,'head'=4] {'seq','head'}, dimensions={0} | all-to-all | bytes 4194304 | tf_op jit(solution)/shard_map/all_to_all | solution.py:119
  182.3 2.0 %reshape.27 = bf16[32,8,4,4,256]{4,3,2,1,0:T(4,128)(2,1)} reshape(bf16[32,128,256]{2,1,0:T(8,128)(2,1)S(1)} %all_to_all.11) | data formatting | bytes 4194304 | tf_op jit(solution)/shard_map/reshape | solution.py:120
  184.3 2.8 %copy.13 = bf16[32,8,4,4,256]{4,3,1,0,2:T(4,128)(2,1)S(1)} copy(bf16[32,8,4,4,256]{4,3,2,1,0:T(4,128)(2,1)} %reshape.27) | data formatting | bytes 4194304 | tf_op jit(solution)/shard_map/reshape | solution.py:120
  187.1 2.0 %reshape.28 = bf16[4,1024,256]{2,1,0:T(8,128)(2,1)} reshape(bf16[4,32,8,4,256]{4,3,2,1,0:T(4,128)(2,1)S(1)} %bitcast.10) | data formatting | bytes 4194304 | tf_op jit(solution)/shard_map/reshape | solution.py:121
  (1 shorter events, 0.0 us)
Async XLA Ops:
  6.5 1.0 copy-start
  6.5 90.5 %all-gather.3.cloned.1.call-start = ((), (), s32[]{:S(2)}) async-start(), calls=%async_computation.2 | async-start | bytes 8650752 | tf_op jit(solution)/shard_map/all_gather | solution.py:96
Sparse Core Ops, SparseCore 0:
  10.2 86.7 all-gather.2
